TPU v7x, 32 devices: a whole 2x2x4 slice. The times are simulated.
32 devices in a mesh: row: 4 (over z), col: 8 (over y, x, core).
Axes of the slice: x: 2, y: 2, z: 4, core: 2. Of those that a mesh axis runs over, the one named last changes fastest.
Arguments:
- features: bfloat16 [64, 131072], P(None, ('row', 'col')), may hold values from -6 to 6
- tile_rows: int32 [4, 8, 512], P('row', 'col'), may hold values from 0 to 255, as said below
- tile_cols: int32 [4, 8, 512], P('row', 'col'), may hold values from 0 to 127
- tile_count: int32 [4, 8], P('row', 'col'), may hold values from 1 to 512, as said below
- tile_data: bfloat16 [4, 8, 512, 128, 128], P('row', 'col'), may hold values from -0.21875 to 0.21875
Outputs:
- filtered: bfloat16 [512, 131072], P(None, ('row', 'col'))
Inputs may be any that keep to these rules, and one draw needn't show every extreme that they name: Within one device the pairs (tile_rows, tile_cols) of all 512 slots are distinct. `tile_count`: some device has all 512 slots live in every draw.
All inputs are finite; a program needn't handle non-finite values.
Results may differ from a plain program's by a relative error of at most 0.009.
Values may be sent and summed in bfloat16 or wider, within the bound.
A program may use at most 128 MiB of HBM per device.

v0:
```python
import functools

import jax
import jax.numpy as jnp
from jax import lax
from jax.experimental import pallas as pl
from jax.experimental.pallas import tpu as pltpu
from jax.sharding import PartitionSpec as P

SCALES = 8
TILE_SIZE = 128
MESH = pl.DeviceIdType.MESH
VMEM = pltpu.VMEM


def bessel_pair(times):
    halved = times / 2.0
    square = halved * halved
    term_zero = jnp.ones_like(times)
    term_one = halved
    sum_zero = term_zero
    sum_one = term_one
    for degree in range(1, 24):
        term_zero = term_zero * square / float(degree * degree)
        term_one = term_one * square / float(degree * (degree + 1))
        sum_zero = sum_zero + term_zero
        sum_one = sum_one + term_one
    damping = jnp.exp(-times)
    return (damping * sum_zero, damping * sum_one)


def coefficients():
    times = 0.25 * 2.0 ** (jnp.arange(SCALES).astype(jnp.float32) / 2.0)
    bessel_zero, bessel_one = bessel_pair(times)
    return (bessel_zero, -2.0 * bessel_one, 2.0 * (bessel_zero - 2.0 * bessel_one / times))


def gather_kernel(count, pieces, field_ref, panel_ref, own_sem, send_sem, recv_sem):
    me = lax.axis_index("row")
    barrier = pltpu.get_barrier_semaphore()
    has_right, has_left = me < count - 1, me > 0

    @pl.when(has_right)
    def _():
        pl.semaphore_signal(barrier, inc=1, device_id={"row": me + 1}, device_id_type=MESH)

    @pl.when(has_left)
    def _():
        pl.semaphore_signal(barrier, inc=1, device_id={"row": me - 1}, device_id_type=MESH)

    own = pltpu.make_async_copy(field_ref, panel_ref.at[me], own_sem)
    own.start()

    inner = jnp.logical_and(has_right, has_left)

    @pl.when(inner)
    def _():
        pl.semaphore_wait(barrier, 2)

    @pl.when(jnp.logical_not(inner))
    def _():
        pl.semaphore_wait(barrier, 1)

    depth = field_ref.shape[0] // pieces

    def transfer(way, step, piece, chunk, source=None):
        rows = pl.ds(piece * depth, depth)
        place = panel_ref.at[chunk, rows]
        return pltpu.make_async_remote_copy(
            src_ref=place if source is None else source.at[rows],
            dst_ref=place,
            send_sem=send_sem.at[way, step, piece],
            recv_sem=recv_sem.at[way, step, piece],
            device_id={"row": me + (1 if way == 0 else -1)},
            device_id_type=MESH,
        )

    for piece in range(pieces):
        for way, can in ((0, has_right), (1, has_left)):
            @pl.when(can)
            def _():
                transfer(way, 0, piece, me, field_ref).start()

    for step in range(1, count):
        for piece in range(pieces):
            for way in range(2):
                arrived = me - step if way == 0 else me + step
                inside = arrived >= 0 if way == 0 else arrived < count
                onward = has_right if way == 0 else has_left

                @pl.when(inside)
                def _():
                    transfer(way, step - 1, piece, arrived).wait_recv()

                if step < count - 1:
                    @pl.when(jnp.logical_and(inside, onward))
                    def _():
                        transfer(way, step, piece, arrived).start()

    own.wait()
    for step in range(count - 1):
        for piece in range(pieces):
            for way in range(2):
                sent = me - step if way == 0 else me + step
                inside = sent >= 0 if way == 0 else sent < count
                onward = has_right if way == 0 else has_left

                @pl.when(jnp.logical_and(inside, onward))
                def _():
                    transfer(way, step, piece, sent).wait_send()


def gather(field, count):
    channels, nodes = field.shape
    pieces = 2
    return pl.pallas_call(
        functools.partial(gather_kernel, count, pieces),
        out_shape=jax.ShapeDtypeStruct((count, channels, nodes), field.dtype),
        in_specs=[pl.BlockSpec(memory_space=VMEM)],
        out_specs=pl.BlockSpec(memory_space=VMEM),
        scratch_shapes=[
            pltpu.SemaphoreType.DMA,
            pltpu.SemaphoreType.DMA((2, count, pieces)),
            pltpu.SemaphoreType.DMA((2, count, pieces)),
        ],
        compiler_params=pltpu.CompilerParams(
            collective_id=0, has_side_effects=True, vmem_limit_bytes=40 * 2**20
        ),
        name="gather",
    )(field)


def bit_orders(count):
    bits = [1 << place for place in range(count.bit_length() - 1)]
    return (bits, bits[:1] + bits[:0:-1])


def scatter_kernel(count, partial_ref, owned_ref, arrived_ref, send_sem, recv_sem):
    me = lax.axis_index("col")
    barrier = pltpu.get_barrier_semaphore()
    orders = bit_orders(count)
    stages = len(orders[0])
    depth = partial_ref.shape[1] // 2

    def side(bit):
        return lax.rem(me // bit, 2)

    def partner(bit):
        return me + bit - 2 * bit * side(bit)

    for bit in orders[0]:
        pl.semaphore_signal(
            barrier, inc=1, device_id={"col": partner(bit)}, device_id_type=MESH
        )
    pl.semaphore_wait(barrier, stages)

    def slot_of(stage, index):
        return (1 << (stages - 1 - stage)) - 1 + index

    def first_block(half, index, away):
        order = orders[half]
        dest = order[0] * (1 - side(order[0]) if away else side(order[0]))
        for place, bit in enumerate(order[1:]):
            differs = (index >> (stages - 2 - place)) & 1
            dest = dest + bit * (1 - side(bit) if differs else side(bit))
        return partial_ref.at[dest, pl.ds(half * depth, depth)]

    def transfer(half, stage, index):
        slot = slot_of(stage, index)
        if stage == 0:
            source = first_block(half, index, True)
        else:
            source = arrived_ref.at[half, slot_of(stage - 1, index + (1 << (stages - 1 - stage)))]
        return pltpu.make_async_remote_copy(
            src_ref=source,
            dst_ref=arrived_ref.at[half, slot],
            send_sem=send_sem.at[half, slot],
            recv_sem=recv_sem.at[half, slot],
            device_id={"col": partner(orders[half][stage])},
            device_id_type=MESH,
        )

    for index in reversed(range(1 << (stages - 1))):
        for half in range(2):
            transfer(half, 0, index).start()

    for stage in range(stages):
        onward = (1 << (stages - 1 - stage)) // 2
        for index in reversed(range(1 << (stages - 1 - stage))):
            for half in range(2):
                transfer(half, stage, index).wait_recv()
                slot = slot_of(stage, index)
                if stage == 0:
                    mine = first_block(half, index, False)[...]
                else:
                    mine = arrived_ref[half, slot_of(stage - 1, index)]
                total = mine + arrived_ref[half, slot]
                if stage == stages - 1:
                    owned_ref[half * depth : (half + 1) * depth] = total
                else:
                    arrived_ref[half, slot] = total
                    if index >= onward:
                        transfer(half, stage + 1, index - onward).start()

    for stage in range(stages):
        for index in range(1 << (stages - 1 - stage)):
            for half in range(2):
                transfer(half, stage, index).wait_send()


def scatter(partial_value):
    count, channels, nodes = partial_value.shape
    return pl.pallas_call(
        functools.partial(scatter_kernel, count),
        out_shape=jax.ShapeDtypeStruct((channels, nodes), partial_value.dtype),
        in_specs=[pl.BlockSpec(memory_space=VMEM)],
        out_specs=pl.BlockSpec(memory_space=VMEM),
        scratch_shapes=[
            pltpu.VMEM((2, count - 1, channels // 2, nodes), partial_value.dtype),
            pltpu.SemaphoreType.DMA((2, count - 1)),
            pltpu.SemaphoreType.DMA((2, count - 1)),
        ],
        compiler_params=pltpu.CompilerParams(
            collective_id=1, has_side_effects=True, vmem_limit_bytes=56 * 2**20
        ),
        name="scatter",
    )(partial_value)


def tile_kernel(block, group, rows_ref, cols_ref, count_ref, panel_ref, data_ref, out_ref, acc_ref):
    step = pl.program_id(0)
    row_blocks = acc_ref.shape[0] - 1
    per_block = panel_ref.shape[2] // TILE_SIZE
    unroll = 8

    @pl.when(step == 0)
    def _():
        def clear(start, carry):
            for offset in range(unroll):
                acc_ref[start * unroll + offset] = jnp.zeros(acc_ref.shape[1:], jnp.float32)
            return carry

        lax.fori_loop(0, row_blocks // unroll, clear, 0)

    live = count_ref[0]

    def one_group(index, carry):
        start = step * block + index * group
        products = []
        for offset in range(group):
            col = cols_ref[start + offset]
            lanes = pl.ds(pl.multiple_of(lax.rem(col, per_block) * TILE_SIZE, TILE_SIZE), TILE_SIZE)
            products.append(
                lax.dot_general(
                    panel_ref[col // per_block, :, lanes],
                    data_ref[index * group + offset],
                    (((1,), (1,)), ((), ())),
                    preferred_element_type=jnp.float32,
                )
            )
        for offset in range(group):
            slot = start + offset
            row = jnp.where(slot < live, rows_ref[slot], row_blocks)
            acc_ref[row] += products[offset]
        return carry

    groups = jnp.clip((live - step * block + group - 1) // group, 0, block // group)
    lax.fori_loop(0, groups, one_group, 0)

    @pl.when(step == pl.num_programs(0) - 1)
    def _():
        per_dest = out_ref.shape[2] // TILE_SIZE

        def finish(dest, carry):
            for offset in range(per_dest):
                out_ref[dest, :, offset * TILE_SIZE : (offset + 1) * TILE_SIZE] = acc_ref[
                    dest * per_dest + offset
                ].astype(out_ref.dtype)
            return carry

        lax.fori_loop(0, out_ref.shape[0], finish, 0)


def tile_products(panel, slot_rows, slot_cols, live_count, slot_data, col_size):
    count, channels, nodes = panel.shape
    slots = slot_rows.shape[0]
    block = min(128, slots)
    group = min(16, block)
    row_blocks = col_size * nodes // TILE_SIZE
    return pl.pallas_call(
        functools.partial(tile_kernel, block, group),
        out_shape=jax.ShapeDtypeStruct((col_size, channels, nodes), panel.dtype),
        grid_spec=pltpu.PrefetchScalarGridSpec(
            num_scalar_prefetch=3,
            grid=(slots // block,),
            in_specs=[
                pl.BlockSpec(panel.shape, lambda i, *_: (0, 0, 0)),
                pl.BlockSpec((block, TILE_SIZE, TILE_SIZE), lambda i, *_: (i, 0, 0)),
            ],
            out_specs=pl.BlockSpec((col_size, channels, nodes), lambda i, *_: (0, 0, 0)),
            scratch_shapes=[pltpu.VMEM((row_blocks + 1, channels, TILE_SIZE), jnp.float32)],
        ),
        compiler_params=pltpu.CompilerParams(
            dimension_semantics=("arbitrary",), vmem_limit_bytes=56 * 2**20
        ),
        name="tiles",
    )(slot_rows, slot_cols, live_count, panel, slot_data)


def shards(features, tile_rows, tile_cols, tile_count, tile_data):
    row_size, col_size = lax.axis_size("row"), lax.axis_size("col")
    node_count = features.shape[1]
    slot_rows = tile_rows.reshape(-1)
    slot_cols = tile_cols.reshape(-1)
    slot_data = tile_data.reshape(-1, TILE_SIZE, TILE_SIZE)
    live_count = tile_count.reshape(-1)

    def apply_operator(field):
        panel = gather(field, row_size)
        partial_value = tile_products(
            panel, slot_rows, slot_cols, live_count, slot_data, col_size
        )
        return scatter(partial_value)

    first = apply_operator(features)
    second = apply_operator(first)
    coef_zero, coef_one, coef_two = coefficients()
    base = features.astype(jnp.float32)
    first_wide = first.astype(jnp.float32)
    second_wide = second.astype(jnp.float32)
    filtered = (
        coef_zero[:, None, None] * base[None]
        + coef_one[:, None, None] * first_wide[None]
        + coef_two[:, None, None] * (2.0 * second_wide - base)[None]
    )
    return filtered.reshape(-1, node_count).astype(jnp.bfloat16)


def solution(mesh):
    return jax.shard_map(
        shards,
        mesh=mesh,
        in_specs=(
            P(None, ("row", "col")),
            P("row", "col", None),
            P("row", "col", None),
            P("row", "col"),
            P("row", "col", None, None, None),
        ),
        out_specs=P(None, ("row", "col")),
        check_vma=False,
    )
```

profile of v0, /device:TPU:0, one launch (start us, length us, event | category | flops | bytes accessed | tf_op | source)
XLA Modules:
  0.0 176.3 jit_solution(2892209563748791613)
XLA Ops:
  0.7 0.0 copy-start.4
  0.7 1.0 copy-done.4
  1.7 39.0 %gather.2.panel_ref = bf16[4,64,4096]{2,1,0:T(8,128)(2,1)S(1)} custom-call(bf16[64,4096]{1,0:T(8,128)(2,1)S(1)} %copy-done.4), custom_call_target="tpu_custom_call" | custom-call | tf_op jit(solution)/shard_map/gather/pallas_call | solution.py:116
  40.8 1.3 copy-done.1
  42.1 16.0 %tiles.2.partial_ref = bf16[8,64,4096]{2,1,0:T(8,128)(2,1)} custom-call(s32[512]{0:T(512)} %bitcast.24, s32[512]{0:T(512)} %bitcast.26, s32[1]{0:T(128)} %bitcast.20.count_ref, bf16[4,64,4096]{2,1,0:T(8,128)(2,1)} %copy-done.1, bf16[512,128,128]{2,1,0:T(8,128)(2,1)} %bitcast.22), custom_call_target="tpu_custom_call" | custom-call | tf_op jit(solution)/shard_map/tiles/pallas_call | solution.py:290
  58.1 28.8 %scatter.2.field_ref = bf16[64,4096]{1,0:T(8,128)(2,1)} custom-call(bf16[8,64,4096]{2,1,0:T(8,128)(2,1)} %tiles.2.partial_ref), custom_call_target="tpu_custom_call" | custom-call | tf_op jit(solution)/shard_map/scatter/pallas_call | solution.py:213
  86.9 1.0 copy-done.2
  88.0 36.5 %gather.3.panel_ref = bf16[4,64,4096]{2,1,0:T(8,128)(2,1)S(1)} custom-call(bf16[64,4096]{1,0:T(8,128)(2,1)S(1)} %copy-done.2), custom_call_target="tpu_custom_call" | custom-call | tf_op jit(solution)/shard_map/gather/pallas_call | solution.py:116
  124.5 1.3 copy-done
  125.8 16.1 %tiles.3.partial_ref = bf16[8,64,4096]{2,1,0:T(8,128)(2,1)} custom-call(s32[512]{0:T(512)} %bitcast.25, s32[512]{0:T(512)} %bitcast.27, s32[1]{0:T(128)} %bitcast.21.count_ref, bf16[4,64,4096]{2,1,0:T(8,128)(2,1)} %copy-done, bf16[512,128,128]{2,1,0:T(8,128)(2,1)} %bitcast.23), custom_call_target="tpu_custom_call" | custom-call | tf_op jit(solution)/shard_map/tiles/pallas_call | solution.py:290
  142.0 28.4 %scatter.3 = bf16[64,4096]{1,0:T(8,128)(2,1)} custom-call(bf16[8,64,4096]{2,1,0:T(8,128)(2,1)} %tiles.3.partial_ref), custom_call_target="tpu_custom_call" | custom-call | tf_op jit(solution)/shard_map/scatter/pallas_call | solution.py:213
  170.4 1.2 multiply_subtract_fusion
  171.6 0.1 convert_element_type.31
  171.7 0.1 convert_element_type.30
  171.8 0.1 add_multiply_fusion.1
  171.8 0.1 mul.710
  171.9 0.1 mul.711
  172.0 0.1 broadcast_multiply_fusion
  172.0 0.1 mul.741
  172.1 0.1 mul.742
  172.2 0.1 subtract_multiply_fusion
  172.3 0.1 mul.749
  172.3 0.1 mul.750
  172.4 3.9 %fusion.1 = bf16[512,4096]{1,0:T(8,128)(2,1)} fusion(f32[64,4096]{1,0:T(8,128)S(1)} %multiply_subtract_fusion, f32[512]{0:T(512)S(1)} %mul.750, f32[64,4096]{1,0:T(8,128)S(1)} %convert_element_type.31, f32[512]{0:T(512)S(1)} %mul.742, f32[64,4096]{1,0:T(8,128)S(1)} %convert_element_type.30, f32[512]{0:T(512)S(1)} %mul.711), kind=kLoop, calls=%fused_computation.2 | loop fusion | flops 12582912 | bytes 7346176 | tf_op jit(solution)/shard_map/convert_element_type | solution.py:336
  (7 shorter events, 0.0 us)
Async XLA Ops:
  0.7 1.0 copy-start.4
  40.7 1.3 copy-start.1
  86.9 1.0 copy-start.2
  124.5 1.3 copy-start
  125.8 44.6 %copy-start.5 = (bf16[64,4096]{1,0:T(8,128)(2,1)S(1)}, bf16[64,4096]{1,0:T(8,128)(2,1)}, u32[]{:S(2)}) copy-start(bf16[64,4096]{1,0:T(8,128)(2,1)} %field_ref.1) | copy-start | bytes 1572868
  125.8 45.8 %copy-start.3 = (bf16[64,4096]{1,0:T(8,128)(2,1)S(1)}, bf16[64,4096]{1,0:T(8,128)(2,1)}, u32[]{:S(2)}) copy-start(bf16[64,4096]{1,0:T(8,128)(2,1)} %scatter.2.field_ref) | copy-start | bytes 1572868
where the time goes:
time: 176 us
  Pallas kernels  165 us (94%)
  other arithmetic  5.42 us (3%)
  local copies, waits for them, and re-layouts  5.19 us (3%)
    pallas_call x2, Pallas kernels, gather(): pl.pallas_call(functools.partial(gather_kernel, count, pieces), out_shape...  75.6 us
    pallas_call x2, Pallas kernels, scatter(): pl.pallas_call(functools.partial(scatter_kernel, count), out_shape=jax.Sh...  57.2 us
    pallas_call x2, Pallas kernels, tile_products(): pl.pallas_call(functools.partial(tile_kernel, block, group), out_shape=ja...  32.2 us
    unnamed x12, local copies, waits for them, and re-layouts  4.75 us
    convert_element_type x1, other arithmetic, shards(): return filtered.reshape(-1, node_count).astype(jnp.bfloat16)  3.91 us

commit v1 on v0

v1 whole, which is shorter than its diff:
```python
import functools

import jax
import jax.numpy as jnp
import numpy as np
from jax import lax
from jax.experimental import pallas as pl
from jax.experimental.pallas import tpu as pltpu
from jax.sharding import PartitionSpec as P

SCALES = 8
TILE = 128
MESH = pl.DeviceIdType.MESH
VMEM = pltpu.VMEM
CHUNKS = (16, 16, 16, 16)
UNROLL = 64
PIECES = 8
REACH = 2


def coefficients():
    times = np.float32(0.25) * np.float32(2.0) ** (np.arange(SCALES).astype(np.float32) / np.float32(2.0))
    halved = times / np.float32(2.0)
    square = halved * halved
    term_zero = np.ones_like(times)
    term_one = halved
    sum_zero, sum_one = term_zero, term_one
    for degree in range(1, 24):
        term_zero = term_zero * square / np.float32(degree * degree)
        term_one = term_one * square / np.float32(degree * (degree + 1))
        sum_zero = sum_zero + term_zero
        sum_one = sum_one + term_one
    damping = np.exp(-times)
    zero, one = damping * sum_zero, damping * sum_one
    return zero, np.float32(-2.0) * one, np.float32(2.0) * (zero - np.float32(2.0) * one / times)


def sign_of(way):
    return 1 - 2 * way


def body(plan, meta_ref, keep_ref, last_ref, features_ref, data_ref, first_ref, second_ref, *scratch):
    row_size, col_size, slots, slot_bits, col_bits = plan
    chunks = len(CHUNKS)
    phases = 2 * chunks
    names = list(scratch)
    panels = [names.pop(0) for _ in range(phases)]
    arrived_a = [names.pop(0) for _ in range(phases)]
    arrived_b = [names.pop(0) for _ in range(phases)]
    partials = [names.pop(0) for _ in range(2)]
    tiles, sums, field, own_sem, tile_sem, zsend, zrecv, asend, arecv, bsend, brecv = names
    width = [CHUNKS[p % chunks] for p in range(phases)]
    start = [sum(CHUNKS[: p % chunks]) for p in range(phases)]
    chips = col_size // 2
    per_block = first_ref.shape[1] // TILE
    row_blocks = col_size * per_block

    me = lax.axis_index("row")
    col = lax.axis_index("col")
    side = lax.rem(col, 2)
    chip = col // 2

    def own_copy(p):
        rows = pl.ds(start[p], width[p])
        return pltpu.make_async_copy(features_ref.at[rows], field.at[rows], own_sem.at[p])

    def tile_copy(piece):
        part = pl.ds(piece * (slots // PIECES), slots // PIECES)
        return pltpu.make_async_copy(data_ref.at[part], tiles.at[part], tile_sem.at[piece])

    for p in range(chunks):
        own_copy(p).start()
    for piece in range(PIECES):
        tile_copy(piece).start()

    barrier = pltpu.get_barrier_semaphore()
    expected = jnp.int32(0)
    for sign in (1, -1):
        for hop in range(1, min(REACH, row_size - 1) + 1):
            peer = me + sign * hop
            inside = jnp.logical_and(peer >= 0, peer < row_size)
            expected = expected + inside.astype(jnp.int32)

            @pl.when(inside)
            def _():
                pl.semaphore_signal(barrier, inc=1, device_id={"row": peer}, device_id_type=MESH)

    pl.semaphore_signal(barrier, inc=1, device_id={"col": col + 1 - 2 * side}, device_id_type=MESH)
    for step in range(1, chips):
        peer = 2 * lax.rem(chip + step, chips) + side
        pl.semaphore_signal(barrier, inc=1, device_id={"col": peer}, device_id_type=MESH)
    pl.semaphore_wait(barrier, expected + chips)

    def zcopy(p, way, hop):
        sign = sign_of(way)
        relayed = hop > REACH
        origin = me - sign * (hop - 1) if relayed else me
        target = me + sign if relayed else me + sign * hop
        inside = jnp.logical_and(target >= 0, target < row_size)
        if relayed:
            inside = jnp.logical_and(inside, jnp.logical_and(origin >= 0, origin < row_size))
        block = panels[p].at[pl.ds(origin * per_block, per_block)]
        copy = pltpu.make_async_remote_copy(
            src_ref=block,
            dst_ref=block,
            send_sem=zsend.at[p, way, hop - 1],
            recv_sem=zrecv.at[p, way, hop - 1],
            device_id={"row": target},
            device_id_type=MESH,
        )
        return inside, copy

    def zarrival(p, way, hop):
        sign = sign_of(way)
        origin = me - sign * hop
        inside = jnp.logical_and(origin >= 0, origin < row_size)
        block = panels[p].at[pl.ds(origin * per_block, per_block)]
        copy = pltpu.make_async_remote_copy(
            src_ref=block,
            dst_ref=block,
            send_sem=zsend.at[p, way, hop - 1],
            recv_sem=zrecv.at[p, way, hop - 1],
            device_id={"row": origin},
            device_id_type=MESH,
        )
        return inside, copy

    def send_own(p):
        for hop in range(min(REACH, row_size - 1), 0, -1):
            for way in range(2):
                inside, copy = zcopy(p, way, hop)
                pl.when(inside)(copy.start)

    def relay(p):
        for hop in range(REACH + 1, row_size):
            for way in range(2):
                inside, copy = zcopy(p, way, hop)
                landed = zarrival(p, way, hop - 1)[1]

                @pl.when(inside)
                def _():
                    landed.wait_recv()
                    copy.start()

    def receive(p):
        for hop in range(1, row_size):
            for way in range(2):
                inside, landed = zarrival(p, way, hop)
                if REACH <= hop < row_size - 1:
                    onward = me + sign_of(way)
                    passes = jnp.logical_and(onward >= 0, onward < row_size)
                    inside = jnp.logical_and(inside, jnp.logical_not(passes))
                pl.when(inside)(landed.wait_recv)

    def products(p, low, high, carry):
        lanes_mask = (1 << col_bits) - 1
        channels = width[p]

        def group(index, total):
            left, right = [], []
            for offset in range(UNROLL):
                word = meta_ref[index * UNROLL + offset]
                column = jnp.bitwise_and(lax.shift_right_logical(word, slot_bits), lanes_mask)
                left.append(panels[p][column])
                right.append(tiles[jnp.bitwise_and(word, slots - 1)])
            parts = []
            for at in range(0, UNROLL, 2):
                both = jnp.dot(
                    jnp.concatenate(left[at : at + 2], 0),
                    jnp.concatenate(right[at : at + 2], 1),
                    preferred_element_type=jnp.float32,
                )
                parts += [both[:channels, :TILE], both[channels:, TILE:]]
            for offset in range(UNROLL):
                total = total * keep_ref[index * UNROLL + offset] + parts[offset]
                sums[1 + index * UNROLL + offset] = total
            return total

        return lax.fori_loop(low, high, group, carry)

    def finish(p):
        channels = width[p]

        def rows(step, carry):
            for offset in range(8):
                at = step * 8 + offset
                dest = at // per_block
                partials[p % 2][lax.rem(dest, 2), dest // 2, lax.rem(at, per_block)] = sums[
                    last_ref[at]
                ].astype(jnp.bfloat16)
            return carry

        lax.fori_loop(0, row_blocks // 8, rows, 0)

    def acopy(p):
        return pltpu.make_async_remote_copy(
            src_ref=partials[p % 2].at[1 - side],
            dst_ref=arrived_a[p],
            send_sem=asend.at[p],
            recv_sem=arecv.at[p],
            device_id={"col": col + 1 - 2 * side},
            device_id_type=MESH,
        )

    def bcopy(p, step):
        target = lax.rem(chip + step, chips)
        return pltpu.make_async_remote_copy(
            src_ref=partials[p % 2].at[side, target],
            dst_ref=arrived_b[p].at[step - 1],
            send_sem=bsend.at[p, step - 1],
            recv_sem=brecv.at[p, step - 1],
            device_id={"col": 2 * target + side},
            device_id_type=MESH,
        )

    def pair_sum(p):
        acopy(p).wait_recv()
        for step in [*range(1, chips), 0]:
            target = lax.rem(chip + step, chips)
            total = partials[p % 2][side, target].astype(jnp.float32) + arrived_a[p][target].astype(jnp.float32)
            partials[p % 2][side, target] = total.astype(jnp.bfloat16)
            if step:
                bcopy(p, step).start()

    def chip_sum(p):
        total = partials[p % 2][side, chip].astype(jnp.float32)
        for step in range(1, chips):
            bcopy(p, step).wait_recv()
            total = total + arrived_b[p][step - 1].astype(jnp.float32)
        result = total.astype(jnp.bfloat16)
        if p < chunks:
            panels[p + chunks][pl.ds(me * per_block, per_block)] = result
            send_own(p + chunks)
        out_ref = first_ref if p < chunks else second_ref
        for block in range(per_block):
            out_ref[start[p] : start[p] + width[p], block * TILE : (block + 1) * TILE] = result[block]

    def settle(p):
        acopy(p).wait_send()
        for step in range(1, chips):
            bcopy(p, step).wait_send()

    for p in range(chunks):
        own_copy(p).wait()
        for block in range(per_block):
            panels[p][me * per_block + block] = field[
                start[p] : start[p] + width[p], block * TILE : (block + 1) * TILE
            ]
        if p < 2:
            send_own(p)

    for piece in range(PIECES):
        tile_copy(piece).wait()

        def turn(step, carry):
            for offset in range(4):
                at = piece * (slots // PIECES) + step * 4 + offset
                tiles[at] = tiles[at].T
            return carry

        lax.fori_loop(0, slots // PIECES // 4, turn, 0)

    sums[0] = jnp.zeros(sums.shape[1:], jnp.float32)

    groups = slots // UNROLL
    relay(0)
    for p in range(phases):
        receive(p)
        carry = jnp.zeros((width[p], TILE), jnp.float32)
        carry = products(p, 0, groups // 2, carry)
        if p >= 1:
            chip_sum(p - 1)
        carry = products(p, groups // 2, groups, carry)
        if p >= 2:
            settle(p - 2)
        finish(p)
        acopy(p).start()
        pair_sum(p)
        if p + 1 < phases:
            relay(p + 1)
        if p + 2 < chunks:
            send_own(p + 2)
    chip_sum(phases - 1)

    for p in (phases - 2, phases - 1):
        settle(p)
    for p in range(phases):
        for way in range(2):
            for hop in range(1, row_size):
                inside, copy = zcopy(p, way, hop)
                pl.when(inside)(copy.wait_send)


def slot_order(slot_rows, slot_cols, live_count, row_blocks, slot_bits, col_bits):
    slots = slot_rows.shape[0]
    index = jnp.arange(slots, dtype=jnp.int32)
    row = jnp.where(index < live_count, slot_rows, row_blocks)
    key = row * slots + index
    rank = jnp.sum((key[None, :] < key[:, None]).astype(jnp.int32), axis=1)
    word = index + (slot_cols << slot_bits) + (row << (slot_bits + col_bits))
    sorted_words = jnp.sum(jnp.where(rank[:, None] == index[None, :], word[:, None], 0), axis=0)
    before = lax.shift_right_logical(jnp.roll(sorted_words, 1), slot_bits + col_bits)
    same = before == lax.shift_right_logical(sorted_words, slot_bits + col_bits)
    keep = jnp.where(jnp.logical_and(same, index > 0), 1.0, 0.0)
    blocks = jnp.arange(row_blocks, dtype=jnp.int32)
    until = jnp.sum((row[:, None] <= blocks[None, :]).astype(jnp.int32), axis=0)
    before = jnp.sum((row[:, None] < blocks[None, :]).astype(jnp.int32), axis=0)
    return sorted_words, keep, jnp.where(until == before, 0, until)


def shards(features, tile_rows, tile_cols, tile_count, tile_data):
    row_size, col_size = lax.axis_size("row"), lax.axis_size("col")
    channels, nodes = features.shape
    slot_rows = tile_rows.reshape(-1)
    slot_cols = tile_cols.reshape(-1)
    slot_data = tile_data.reshape(-1, TILE, TILE)
    slots = slot_rows.shape[0]
    row_blocks = col_size * nodes // TILE
    slot_bits = (slots - 1).bit_length()
    col_bits = (row_size * nodes // TILE - 1).bit_length()
    words, keep, last = slot_order(
        slot_rows, slot_cols, tile_count.reshape(()), row_blocks, slot_bits, col_bits
    )
    phases = 2 * len(CHUNKS)
    chips = col_size // 2
    widths = [CHUNKS[p % len(CHUNKS)] for p in range(phases)]
    field = jax.ShapeDtypeStruct((channels, nodes), jnp.bfloat16)
    dma = pltpu.SemaphoreType.DMA
    wide = max(CHUNKS)
    per_block = nodes // TILE
    scratch = [VMEM((row_size * per_block, w, TILE), jnp.bfloat16) for w in widths]
    scratch += [VMEM((chips, per_block, w, TILE), jnp.bfloat16) for w in widths]
    scratch += [VMEM((chips - 1, per_block, w, TILE), jnp.bfloat16) for w in widths]
    scratch += [VMEM((2, chips, per_block, wide, TILE), jnp.bfloat16)] * 2
    scratch += [
        VMEM((slots, TILE, TILE), jnp.bfloat16),
        VMEM((slots + 1, wide, TILE), jnp.float32),
        VMEM((channels, nodes), jnp.bfloat16),
        dma((len(CHUNKS),)),
        dma((PIECES,)),
        dma((phases, 2, row_size - 1)),
        dma((phases, 2, row_size - 1)),
        dma((phases,)),
        dma((phases,)),
        dma((phases, chips - 1)),
        dma((phases, chips - 1)),
    ]
    first, second = pl.pallas_call(
        functools.partial(body, (row_size, col_size, slots, slot_bits, col_bits)),
        out_shape=(field, field),
        in_specs=[
            pl.BlockSpec(memory_space=pltpu.SMEM),
            pl.BlockSpec(memory_space=pltpu.SMEM),
            pl.BlockSpec(memory_space=pltpu.SMEM),
            pl.BlockSpec(memory_space=pl.ANY),
            pl.BlockSpec(memory_space=pl.ANY),
        ],
        out_specs=(pl.BlockSpec(memory_space=VMEM), pl.BlockSpec(memory_space=VMEM)),
        scratch_shapes=scratch,
        compiler_params=pltpu.CompilerParams(
            collective_id=0, has_side_effects=True, vmem_limit_bytes=60 * 2**20
        ),
        name="operator_twice",
    )(words, keep, last, features, slot_data)

    coef_zero, coef_one, coef_two = coefficients()
    base = features.astype(jnp.float32)
    first_wide = first.astype(jnp.float32)
    second_wide = second.astype(jnp.float32)
    filtered = (
        coef_zero[:, None, None] * base[None]
        + coef_one[:, None, None] * first_wide[None]
        + coef_two[:, None, None] * (2.0 * second_wide - base)[None]
    )
    return filtered.reshape(-1, nodes).astype(jnp.bfloat16)


def solution(mesh):
    return jax.shard_map(
        shards,
        mesh=mesh,
        in_specs=(
            P(None, ("row", "col")),
            P("row", "col", None),
            P("row", "col", None),
            P("row", "col"),
            P("row", "col", None, None, None),
        ),
        out_specs=P(None, ("row", "col")),
        check_vma=False,
    )
```

time: 176 us -> 161 us (0.915)
  Pallas kernels: 165 us -> 146 us
  other arithmetic: 5.42 us -> 10.3 us
  local copies, waits for them, and re-layouts: 5.19 us -> 3.07 us
    pallas_call x6 -> x1, Pallas kernels: 165 us -> 146 us  [shards(): pl.pallas_call(functools.partial(body, (row_size, col_size, slots, slot_b...]
    unnamed x12 -> x4, local copies, waits for them, and re-layouts: 4.75 us -> 0.01 us
    select_n x0 -> x2, other arithmetic: none -> 1.95 us  [the longest x1 1.35 us: slot_order(): keep = jnp.where(jnp.logical_and(same, index > 0), 1.0, 0.0)]
where the time goes in v1:
time: 161 us; the launch traced here: 160 us
  Pallas kernels  146 us (91%)
  other arithmetic  10.3 us (6%)
  local copies, waits for them, and re-layouts  3.07 us (2%)
    pallas_call x1, Pallas kernels, shards(): pl.pallas_call(functools.partial(body, (row_size, col_size, slots, slot_b...  146 us
    convert_element_type x1, other arithmetic, shards(): return filtered.reshape(-1, nodes).astype(jnp.bfloat16)  3.93 us

profile of v1, /device:TPU:0, one launch (start us, length us, event | category | flops | bytes accessed | tf_op | source)
XLA Modules:
  0.0 160.3 jit_solution(723328877634032405)
XLA Ops:
  0.7 0.7 broadcast_shift-left_fusion
  1.3 0.7 iota_add_fusion
  2.0 0.2 convert_reduce_fusion
  2.3 0.2 select_reduce_fusion.meta_ref
  2.5 0.0 copy-start.1
  2.5 0.7 slice.8
  3.2 0.2 convert_reduce_fusion.1
  3.4 0.6 compare_select_fusion.last_ref
  4.0 1.4 fusion.6.keep_ref
  5.3 0.7 mul.87
  6.0 0.1 mul.88
  6.1 0.7 mul.94
  6.8 0.1 mul.95
  6.9 0.7 mul.103
  7.6 0.1 mul.104
  7.7 0.0 copy-done.1
  7.7 0.0 copy-start
  7.7 146.3 %operator_twice.1 = (bf16[64,4096]{1,0:T(8,128)(2,1)}, bf16[64,4096]{1,0:T(8,128)(2,1)}) custom-call(s32[512]{0:T(512)} %copy-done.1, f32[512]{0:T(512)} %fusion.6.keep_ref, s32[256]{0:T(256)} %compare_select_fusion.last_ref, bf16[64,4096]{1,0:T(8,128)(2,1)} %features_ref.1, bf16[512,128,128]{2,1,0:T(8,128)(2,1)} %bitcast.22), custom_call_target="tpu_custom_call" | custom-call | tf_op jit(solution)/shard_map/operator_twice/pallas_call | solution.py:348
  154.0 1.1 convert_element_type.25
  155.1 0.0 copy-done
  155.1 1.2 multiply_subtract_fusion
  156.3 0.1 convert_element_type.21
  156.4 3.9 %fusion.1 = bf16[512,4096]{1,0:T(8,128)(2,1)} fusion(f32[64,4096]{1,0:T(8,128)S(1)} %multiply_subtract_fusion, f32[512]{0:T(512)S(1)} %mul.104, f32[64,4096]{1,0:T(8,128)S(1)} %convert_element_type.25, f32[512]{0:T(512)S(1)} %mul.95, f32[64,4096]{1,0:T(8,128)S(1)} %convert_element_type.21, f32[512]{0:T(512)S(1)} %mul.88), kind=kLoop, calls=%fused_computation.2 | loop fusion | flops 12582912 | bytes 7346176 | tf_op jit(solution)/shard_map/convert_element_type | solution.py:375
  (1 shorter events, 0.0 us)
Async XLA Ops:
  2.5 5.2 %copy-start.1 = (s32[512]{0:T(512)}, s32[512]{0:T(512)S(1)}, u32[]{:S(2)}) copy-start(s32[512]{0:T(512)S(1)} %select_reduce_fusion.meta_ref) | copy-start | bytes 6148
  7.7 147.4 %copy-start = (bf16[64,4096]{1,0:T(8,128)(2,1)S(1)}, bf16[64,4096]{1,0:T(8,128)(2,1)}, u32[]{:S(2)}) copy-start(bf16[64,4096]{1,0:T(8,128)(2,1)} %features_ref.1) | copy-start | bytes 1572868

commit v2 on v1

--- a/solution.py
+++ b/solution.py
@@ -13,9 +13,10 @@
 MESH = pl.DeviceIdType.MESH
 VMEM = pltpu.VMEM
 CHUNKS = (16, 16, 16, 16)
-UNROLL = 64
+UNROLL = TILE
 PIECES = 8
 REACH = 2
+AHEAD = 3
 
 
 def coefficients():
@@ -39,7 +40,7 @@
     return 1 - 2 * way
 
 
-def body(plan, meta_ref, keep_ref, last_ref, features_ref, data_ref, first_ref, second_ref, *scratch):
+def body(plan, rows_ref, cols_ref, count_ref, features_ref, data_ref, first_ref, second_ref, *scratch):
     row_size, col_size, slots, slot_bits, col_bits = plan
     chunks = len(CHUNKS)
     phases = 2 * chunks
@@ -48,7 +49,7 @@
     arrived_a = [names.pop(0) for _ in range(phases)]
     arrived_b = [names.pop(0) for _ in range(phases)]
     partials = [names.pop(0) for _ in range(2)]
-    tiles, sums, field, own_sem, tile_sem, zsend, zrecv, asend, arecv, bsend, brecv = names
+    tiles, sums, field, words, keeps, lasts, meta_ref, keep_ref, last_ref, order_sem, own_sem, tile_sem, zsend, zrecv, asend, arecv, bsend, brecv = names
     width = [CHUNKS[p % chunks] for p in range(phases)]
     start = [sum(CHUNKS[: p % chunks]) for p in range(phases)]
     chips = col_size // 2
@@ -91,75 +92,90 @@
         pl.semaphore_signal(barrier, inc=1, device_id={"col": peer}, device_id_type=MESH)
     pl.semaphore_wait(barrier, expected + chips)
 
-    def zcopy(p, way, hop):
-        sign = sign_of(way)
-        relayed = hop > REACH
-        origin = me - sign * (hop - 1) if relayed else me
-        target = me + sign if relayed else me + sign * hop
-        inside = jnp.logical_and(target >= 0, target < row_size)
-        if relayed:
-            inside = jnp.logical_and(inside, jnp.logical_and(origin >= 0, origin < row_size))
+    def within(at):
+        return jnp.logical_and(at >= 0, at < row_size)
+
+    def last_of(way):
+        return row_size - 1 if way == 0 else 0
+
+    def zcopy(p, way, hop, origin, target, place=0):
         block = panels[p].at[pl.ds(origin * per_block, per_block)]
-        copy = pltpu.make_async_remote_copy(
+        return pltpu.make_async_remote_copy(
             src_ref=block,
             dst_ref=block,
-            send_sem=zsend.at[p, way, hop - 1],
+            send_sem=zsend.at[p, way, place + hop - 1],
             recv_sem=zrecv.at[p, way, hop - 1],
             device_id={"row": target},
             device_id_type=MESH,
         )
-        return inside, copy
-
-    def zarrival(p, way, hop):
-        sign = sign_of(way)
-        origin = me - sign * hop
-        inside = jnp.logical_and(origin >= 0, origin < row_size)
-        block = panels[p].at[pl.ds(origin * per_block, per_block)]
-        copy = pltpu.make_async_remote_copy(
-            src_ref=block,
-            dst_ref=block,
-            send_sem=zsend.at[p, way, hop - 1],
-            recv_sem=zrecv.at[p, way, hop - 1],
-            device_id={"row": origin},
-            device_id_type=MESH,
-        )
-        return inside, copy
+
+    def direct(p, way, hop):
+        target = me + sign_of(way) * hop
+        inside = within(target)
+        if hop > 1:
+            inside = jnp.logical_and(inside, target != last_of(way))
+        return inside, zcopy(p, way, hop, me, target)
+
+    def relayed(p, way, hop):
+        target = me + sign_of(way)
+        origin = target - sign_of(way) * hop
+        inside = jnp.logical_and(within(target), within(origin))
+        if hop <= REACH:
+            inside = jnp.logical_and(inside, target == last_of(way))
+        return inside, zcopy(p, way, hop, origin, target, row_size)
+
+    def landed(p, way, hop):
+        origin = me - sign_of(way) * hop
+        return within(origin), zcopy(p, way, hop, origin, origin)
+
+    direct_hops = range(min(REACH, row_size - 1), 0, -1)
+    relay_hops = range(2, row_size)
 
     def send_own(p):
-        for hop in range(min(REACH, row_size - 1), 0, -1):
+        for hop in direct_hops:
             for way in range(2):
-                inside, copy = zcopy(p, way, hop)
+                inside, copy = direct(p, way, hop)
                 pl.when(inside)(copy.start)
 
     def relay(p):
-        for hop in range(REACH + 1, row_size):
+        for hop in relay_hops:
             for way in range(2):
-                inside, copy = zcopy(p, way, hop)
-                landed = zarrival(p, way, hop - 1)[1]
+                inside, copy = relayed(p, way, hop)
+                arrival = landed(p, way, hop - 1)[1]
 
                 @pl.when(inside)
                 def _():
-                    landed.wait_recv()
+                    arrival.wait_recv()
                     copy.start()
 
     def receive(p):
         for hop in range(1, row_size):
             for way in range(2):
-                inside, landed = zarrival(p, way, hop)
-                if REACH <= hop < row_size - 1:
-                    onward = me + sign_of(way)
-                    passes = jnp.logical_and(onward >= 0, onward < row_size)
-                    inside = jnp.logical_and(inside, jnp.logical_not(passes))
-                pl.when(inside)(landed.wait_recv)
-
-    def products(p, low, high, carry):
+                inside, arrival = landed(p, way, hop)
+                target = me + sign_of(way)
+                passes = within(target)
+                if hop + 1 <= REACH:
+                    passes = jnp.logical_and(passes, target == last_of(way))
+                inside = jnp.logical_and(inside, jnp.logical_not(passes))
+                pl.when(inside)(arrival.wait_recv)
+
+    def sent(p):
+        for way in range(2):
+            for hop in direct_hops:
+                inside, copy = direct(p, way, hop)
+                pl.when(inside)(copy.wait_send)
+            for hop in relay_hops:
+                inside, copy = relayed(p, way, hop)
+                pl.when(inside)(copy.wait_send)
+
+    def products(p):
         lanes_mask = (1 << col_bits) - 1
         channels = width[p]
 
         def group(index, total):
             left, right = [], []
             for offset in range(UNROLL):
-                word = meta_ref[index * UNROLL + offset]
+                word = meta_ref[index, offset]
                 column = jnp.bitwise_and(lax.shift_right_logical(word, slot_bits), lanes_mask)
                 left.append(panels[p][column])
                 right.append(tiles[jnp.bitwise_and(word, slots - 1)])
@@ -172,25 +188,24 @@
                 )
                 parts += [both[:channels, :TILE], both[channels:, TILE:]]
             for offset in range(UNROLL):
-                total = total * keep_ref[index * UNROLL + offset] + parts[offset]
+                total = total * keep_ref[index, offset] + parts[offset]
                 sums[1 + index * UNROLL + offset] = total
             return total
 
-        return lax.fori_loop(low, high, group, carry)
+        empty = jnp.zeros((channels, TILE), jnp.float32)
+        lax.fori_loop(0, slots // UNROLL, group, empty)
 
     def finish(p):
-        channels = width[p]
-
-        def rows(step, carry):
-            for offset in range(8):
-                at = step * 8 + offset
-                dest = at // per_block
-                partials[p % 2][lax.rem(dest, 2), dest // 2, lax.rem(at, per_block)] = sums[
-                    last_ref[at]
+        def rows(dest, carry):
+            chip_of, side_of = dest // 2, lax.rem(dest, 2)
+            line, first_at = dest * per_block // TILE, lax.rem(dest * per_block, TILE)
+            for block in range(per_block):
+                partials[p % 2][side_of, chip_of, block] = sums[
+                    last_ref[line, first_at + block]
                 ].astype(jnp.bfloat16)
             return carry
 
-        lax.fori_loop(0, row_blocks // 8, rows, 0)
+        lax.fori_loop(0, col_size, rows, 0)
 
     def acopy(p):
         return pltpu.make_async_remote_copy(
@@ -246,8 +261,65 @@
             panels[p][me * per_block + block] = field[
                 start[p] : start[p] + width[p], block * TILE : (block + 1) * TILE
             ]
-        if p < 2:
+        if p < AHEAD:
             send_own(p)
+
+    def order():
+        live = count_ref[0, 0]
+        square = (TILE, TILE)
+        lane = lax.broadcasted_iota(jnp.int32, square, 1)
+        none = jnp.zeros(square, jnp.int32)
+        keys, rows_lane, keys_down, rows_down, words_down = [], [], [], [], []
+        pieces = slots // TILE
+        for piece in range(pieces):
+            part = slice(piece * TILE, (piece + 1) * TILE)
+            index = lane + piece * TILE
+            row = jnp.where(index < live, jnp.broadcast_to(rows_ref[0, :, part], square), row_blocks)
+            word = index + jnp.broadcast_to(cols_ref[0, :, part], square) * slots
+            keys.append(row * slots + index)
+            rows_lane.append(row)
+            keys_down.append(keys[-1].T)
+            rows_down.append(row.T)
+            words_down.append(word.T)
+        ranks, repeats = [], []
+        for piece in range(pieces):
+            ahead, same = none, none
+            for other in range(pieces):
+                less = jnp.where(keys_down[other] < keys[piece], 1, 0)
+                ahead = ahead + less
+                same = same + jnp.where(rows_down[other] == rows_lane[piece], less, 0)
+            ahead = jnp.sum(ahead, axis=0, keepdims=True)
+            same = jnp.minimum(jnp.sum(same, axis=0, keepdims=True), 1)
+            ranks.append(jnp.broadcast_to(ahead, square).T)
+            repeats.append(jnp.broadcast_to(same, square).T)
+        for piece in range(pieces):
+            place = lane + piece * TILE
+            word, keep = none, none
+            for other in range(pieces):
+                here = ranks[other] == place
+                word = word + jnp.where(here, words_down[other], 0)
+                keep = keep + jnp.where(here, repeats[other], 0)
+            words[piece : piece + 1] = jnp.sum(word, axis=0, keepdims=True)
+            keeps[piece : piece + 1] = jnp.sum(keep, axis=0, keepdims=True).astype(jnp.float32)
+        for piece in range(row_blocks // TILE):
+            place = lane + piece * TILE
+            until, before = none, none
+            for other in range(pieces):
+                until = until + jnp.where(rows_down[other] <= place, 1, 0)
+                before = before + jnp.where(rows_down[other] < place, 1, 0)
+            until = jnp.sum(until, axis=0, keepdims=True)
+            before = jnp.sum(before, axis=0, keepdims=True)
+            lasts[piece : piece + 1] = jnp.where(until == before, 0, until)
+        moves = [
+            pltpu.make_async_copy(source, target, order_sem.at[at])
+            for at, (source, target) in enumerate(((words, meta_ref), (keeps, keep_ref), (lasts, last_ref)))
+        ]
+        for move in moves:
+            move.start()
+        for move in moves:
+            move.wait()
+
+    order()
 
     for piece in range(PIECES):
         tile_copy(piece).wait()
@@ -259,68 +331,51 @@
             return carry
 
         lax.fori_loop(0, slots // PIECES // 4, turn, 0)
+        if piece == PIECES // 2:
+            relay(0)
+            if chunks > AHEAD:
+                send_own(AHEAD)
 
     sums[0] = jnp.zeros(sums.shape[1:], jnp.float32)
 
-    groups = slots // UNROLL
-    relay(0)
     for p in range(phases):
         receive(p)
-        carry = jnp.zeros((width[p], TILE), jnp.float32)
-        carry = products(p, 0, groups // 2, carry)
-        if p >= 1:
-            chip_sum(p - 1)
-        carry = products(p, groups // 2, groups, carry)
+        if p + 1 < phases:
+            relay(p + 1)
+        if p + 1 + AHEAD < chunks:
+            send_own(p + 1 + AHEAD)
+        products(p)
         if p >= 2:
             settle(p - 2)
         finish(p)
         acopy(p).start()
         pair_sum(p)
-        if p + 1 < phases:
-            relay(p + 1)
-        if p + 2 < chunks:
-            send_own(p + 2)
+        if p >= 1:
+            chip_sum(p - 1)
     chip_sum(phases - 1)
 
     for p in (phases - 2, phases - 1):
         settle(p)
     for p in range(phases):
-        for way in range(2):
-            for hop in range(1, row_size):
-                inside, copy = zcopy(p, way, hop)
-                pl.when(inside)(copy.wait_send)
-
-
-def slot_order(slot_rows, slot_cols, live_count, row_blocks, slot_bits, col_bits):
-    slots = slot_rows.shape[0]
-    index = jnp.arange(slots, dtype=jnp.int32)
-    row = jnp.where(index < live_count, slot_rows, row_blocks)
-    key = row * slots + index
-    rank = jnp.sum((key[None, :] < key[:, None]).astype(jnp.int32), axis=1)
-    word = index + (slot_cols << slot_bits) + (row << (slot_bits + col_bits))
-    sorted_words = jnp.sum(jnp.where(rank[:, None] == index[None, :], word[:, None], 0), axis=0)
-    before = lax.shift_right_logical(jnp.roll(sorted_words, 1), slot_bits + col_bits)
-    same = before == lax.shift_right_logical(sorted_words, slot_bits + col_bits)
-    keep = jnp.where(jnp.logical_and(same, index > 0), 1.0, 0.0)
-    blocks = jnp.arange(row_blocks, dtype=jnp.int32)
-    until = jnp.sum((row[:, None] <= blocks[None, :]).astype(jnp.int32), axis=0)
-    before = jnp.sum((row[:, None] < blocks[None, :]).astype(jnp.int32), axis=0)
-    return sorted_words, keep, jnp.where(until == before, 0, until)
+        sent(p)
+
+
+def filter_bank(coefs, base_ref, first_ref, second_ref, out_ref):
+    base = base_ref[...].astype(jnp.float32)
+    first = first_ref[...].astype(jnp.float32)
+    rest = 2.0 * second_ref[...].astype(jnp.float32) - base
+    for scale, (zero, one, two) in enumerate(coefs):
+        out_ref[scale] = (zero * base + one * first + two * rest).astype(out_ref.dtype)
 
 
 def shards(features, tile_rows, tile_cols, tile_count, tile_data):
     row_size, col_size = lax.axis_size("row"), lax.axis_size("col")
     channels, nodes = features.shape
-    slot_rows = tile_rows.reshape(-1)
-    slot_cols = tile_cols.reshape(-1)
-    slot_data = tile_data.reshape(-1, TILE, TILE)
-    slots = slot_rows.shape[0]
+    slots = tile_rows.shape[2]
+    slot_data = tile_data.reshape(slots, TILE, TILE)
     row_blocks = col_size * nodes // TILE
     slot_bits = (slots - 1).bit_length()
     col_bits = (row_size * nodes // TILE - 1).bit_length()
-    words, keep, last = slot_order(
-        slot_rows, slot_cols, tile_count.reshape(()), row_blocks, slot_bits, col_bits
-    )
     phases = 2 * len(CHUNKS)
     chips = col_size // 2
     widths = [CHUNKS[p % len(CHUNKS)] for p in range(phases)]
@@ -336,10 +391,17 @@
         VMEM((slots, TILE, TILE), jnp.bfloat16),
         VMEM((slots + 1, wide, TILE), jnp.float32),
         VMEM((channels, nodes), jnp.bfloat16),
+        VMEM((slots // TILE, TILE), jnp.int32),
+        VMEM((slots // TILE, TILE), jnp.float32),
+        VMEM((row_blocks // TILE, TILE), jnp.int32),
+        pltpu.SMEM((slots // TILE, TILE), jnp.int32),
+        pltpu.SMEM((slots // TILE, TILE), jnp.float32),
+        pltpu.SMEM((row_blocks // TILE, TILE), jnp.int32),
+        dma((3,)),
         dma((len(CHUNKS),)),
         dma((PIECES,)),
-        dma((phases, 2, row_size - 1)),
-        dma((phases, 2, row_size - 1)),
+        dma((phases, 2, 2 * row_size)),
+        dma((phases, 2, row_size)),
         dma((phases,)),
         dma((phases,)),
         dma((phases, chips - 1)),
@@ -349,8 +411,8 @@
         functools.partial(body, (row_size, col_size, slots, slot_bits, col_bits)),
         out_shape=(field, field),
         in_specs=[
-            pl.BlockSpec(memory_space=pltpu.SMEM),
-            pl.BlockSpec(memory_space=pltpu.SMEM),
+            pl.BlockSpec(memory_space=VMEM),
+            pl.BlockSpec(memory_space=VMEM),
             pl.BlockSpec(memory_space=pltpu.SMEM),
             pl.BlockSpec(memory_space=pl.ANY),
             pl.BlockSpec(memory_space=pl.ANY),
@@ -361,18 +423,20 @@
             collective_id=0, has_side_effects=True, vmem_limit_bytes=60 * 2**20
         ),
         name="operator_twice",
-    )(words, keep, last, features, slot_data)
-
-    coef_zero, coef_one, coef_two = coefficients()
-    base = features.astype(jnp.float32)
-    first_wide = first.astype(jnp.float32)
-    second_wide = second.astype(jnp.float32)
-    filtered = (
-        coef_zero[:, None, None] * base[None]
-        + coef_one[:, None, None] * first_wide[None]
-        + coef_two[:, None, None] * (2.0 * second_wide - base)[None]
-    )
-    return filtered.reshape(-1, nodes).astype(jnp.bfloat16)
+    )(tile_rows, tile_cols, tile_count, features, slot_data)
+
+    depth = 16
+    coefs = [tuple(float(c) for c in row) for row in zip(*coefficients())]
+    rows = pl.BlockSpec((depth, nodes), lambda i: (i, 0))
+    filtered = pl.pallas_call(
+        functools.partial(filter_bank, coefs),
+        out_shape=jax.ShapeDtypeStruct((SCALES, channels, nodes), jnp.bfloat16),
+        grid=(channels // depth,),
+        in_specs=[rows, rows, rows],
+        out_specs=pl.BlockSpec((SCALES, depth, nodes), lambda i: (0, i, 0)),
+        name="filter_bank",
+    )(features, first, second)
+    return filtered.reshape(SCALES * channels, nodes)
 
 
 def solution(mesh):

time: 161 us -> 99.9 us (0.62)
  Pallas kernels: 146 us -> 99.1 us
  other arithmetic: 10.3 us -> 0 us
  local copies, waits for them, and re-layouts: 3.07 us -> 0 us
    pallas_call x1, Pallas kernels: 146 us -> 94.1 us  [shards(): pl.pallas_call(functools.partial(body, (row_size, col_size, slots, slot_b...]
    convert_element_type x3 -> x0, other arithmetic: 5.11 us -> none  [the longest x1 3.93 us: shards(): return filtered.reshape(-1, nodes).astype(jnp.bfloat16)]
    pallas_call x0 -> x1, Pallas kernels: none -> 4.97 us  [shards(): pl.pallas_call(functools.partial(filter_bank, coefs), out_shape=jax.Shape...]
    mul x6 -> x0, local copies, waits for them, and re-layouts: 2.4 us -> none  [the longest x2 0.8 us: shards(): coef_zero[:, None, None] * base[None]]
    select_n x2 -> x0, other arithmetic: 1.95 us -> none  [the longest x1 1.35 us: slot_order(): keep = jnp.where(jnp.logical_and(same, index > 0), 1.0, 0.0)]
where the time goes in v2:
time: 99.9 us; the launch traced here: 99.7 us
  Pallas kernels  99.1 us (99%)
    pallas_call x1, Pallas kernels, shards(): pl.pallas_call(functools.partial(body, (row_size, col_size, slots, slot_b...  94.1 us
    pallas_call x1, Pallas kernels, shards(): pl.pallas_call(functools.partial(filter_bank, coefs), out_shape=jax.Shape...  4.97 us

profile of v2, /device:TPU:0, one launch (start us, length us, event | category | flops | bytes accessed | tf_op | source)
XLA Modules:
  0.0 99.7 jit_solution(15015138045635206998)
XLA Ops:
  0.7 94.1 %operator_twice.1 = (bf16[64,4096]{1,0:T(8,128)(2,1)}, bf16[64,4096]{1,0:T(8,128)(2,1)}) custom-call(s32[1,1,512]{2,1,0:T(1,128)} %rows_ref.1, s32[1,1,512]{2,1,0:T(1,128)} %cols_ref.1, s32[1,1]{1,0:T(1,128)S(6)} %copy.6.count_ref, bf16[64,4096]{1,0:T(8,128)(2,1)} %base_ref.1, bf16[512,128,128]{2,1,0:T(8,128)(2,1)} %bitcast.2), custom_call_target="tpu_custom_call" | custom-call | tf_op jit(solution)/shard_map/operator_twice/pallas_call | solution.py:410
  94.7 5.0 %filter_bank.1 = bf16[8,64,4096]{2,1,0:T(8,128)(2,1)} custom-call(bf16[64,4096]{1,0:T(8,128)(2,1)} %base_ref.1, bf16[64,4096]{1,0:T(8,128)(2,1)} %get-tuple-element.7.first_ref, bf16[64,4096]{1,0:T(8,128)(2,1)} %get-tuple-element.8.second_ref), custom_call_target="tpu_custom_call" | custom-call | tf_op jit(solution)/shard_map/filter_bank/pallas_call | solution.py:431

commit v3 on v2

--- a/solution.py
+++ b/solution.py
@@ -16,7 +16,7 @@
 UNROLL = TILE
 PIECES = 8
 REACH = 2
-AHEAD = 3
+AHEAD = 4
 
 
 def coefficients():
@@ -48,10 +48,13 @@
     panels = [names.pop(0) for _ in range(phases)]
     arrived_a = [names.pop(0) for _ in range(phases)]
     arrived_b = [names.pop(0) for _ in range(phases)]
-    partials = [names.pop(0) for _ in range(2)]
-    tiles, sums, field, words, keeps, lasts, meta_ref, keep_ref, last_ref, order_sem, own_sem, tile_sem, zsend, zrecv, asend, arecv, bsend, brecv = names
+    kinds = sorted(set(CHUNKS))
+    by_kind = {w: (names.pop(0), names.pop(0), names.pop(0)) for w in kinds}
+    tiles, field, words, keeps, lasts, meta_ref, keep_ref, last_ref, order_sem, own_sem, tile_sem, zsend, zrecv, asend, arecv, bsend, brecv = names
     width = [CHUNKS[p % chunks] for p in range(phases)]
     start = [sum(CHUNKS[: p % chunks]) for p in range(phases)]
+    partials = [by_kind[width[p]][p % 2] for p in range(phases)]
+    sums = [by_kind[width[p]][2] for p in range(phases)]
     chips = col_size // 2
     per_block = first_ref.shape[1] // TILE
     row_blocks = col_size * per_block
@@ -189,30 +192,40 @@
                 parts += [both[:channels, :TILE], both[channels:, TILE:]]
             for offset in range(UNROLL):
                 total = total * keep_ref[index, offset] + parts[offset]
-                sums[1 + index * UNROLL + offset] = total
+                sums[p][1 + index * UNROLL + offset] = total
             return total
 
         empty = jnp.zeros((channels, TILE), jnp.float32)
         lax.fori_loop(0, slots // UNROLL, group, empty)
 
     def finish(p):
-        def rows(dest, carry):
-            chip_of, side_of = dest // 2, lax.rem(dest, 2)
+        def rows(target, side_of):
+            dest = 2 * target + side_of
             line, first_at = dest * per_block // TILE, lax.rem(dest * per_block, TILE)
             for block in range(per_block):
-                partials[p % 2][side_of, chip_of, block] = sums[
+                partials[p][side_of, target, block] = sums[p][
                     last_ref[line, first_at + block]
                 ].astype(jnp.bfloat16)
+
+        def given(step, carry):
+            target = lax.rem(chip + step, chips)
+            rows(target, 1 - side)
+            acopy(p, target).start()
             return carry
 
-        lax.fori_loop(0, col_size, rows, 0)
-
-    def acopy(p):
+        def kept(target, carry):
+            rows(target, side)
+            return carry
+
+        lax.fori_loop(1, chips + 1, given, 0)
+        lax.fori_loop(0, chips, kept, 0)
+
+    def acopy(p, target):
         return pltpu.make_async_remote_copy(
-            src_ref=partials[p % 2].at[1 - side],
-            dst_ref=arrived_a[p],
-            send_sem=asend.at[p],
-            recv_sem=arecv.at[p],
+            src_ref=partials[p].at[1 - side, target],
+            dst_ref=arrived_a[p].at[target],
+            send_sem=asend.at[p, target],
+            recv_sem=arecv.at[p, target],
             device_id={"col": col + 1 - 2 * side},
             device_id_type=MESH,
         )
@@ -220,7 +233,7 @@
     def bcopy(p, step):
         target = lax.rem(chip + step, chips)
         return pltpu.make_async_remote_copy(
-            src_ref=partials[p % 2].at[side, target],
+            src_ref=partials[p].at[side, target],
             dst_ref=arrived_b[p].at[step - 1],
             send_sem=bsend.at[p, step - 1],
             recv_sem=brecv.at[p, step - 1],
@@ -229,16 +242,16 @@
         )
 
     def pair_sum(p):
-        acopy(p).wait_recv()
         for step in [*range(1, chips), 0]:
             target = lax.rem(chip + step, chips)
-            total = partials[p % 2][side, target].astype(jnp.float32) + arrived_a[p][target].astype(jnp.float32)
-            partials[p % 2][side, target] = total.astype(jnp.bfloat16)
+            acopy(p, target).wait_recv()
+            total = partials[p][side, target].astype(jnp.float32) + arrived_a[p][target].astype(jnp.float32)
+            partials[p][side, target] = total.astype(jnp.bfloat16)
             if step:
                 bcopy(p, step).start()
 
     def chip_sum(p):
-        total = partials[p % 2][side, chip].astype(jnp.float32)
+        total = partials[p][side, chip].astype(jnp.float32)
         for step in range(1, chips):
             bcopy(p, step).wait_recv()
             total = total + arrived_b[p][step - 1].astype(jnp.float32)
@@ -251,7 +264,8 @@
             out_ref[start[p] : start[p] + width[p], block * TILE : (block + 1) * TILE] = result[block]
 
     def settle(p):
-        acopy(p).wait_send()
+        for target in range(chips):
+            acopy(p, target).wait_send()
         for step in range(1, chips):
             bcopy(p, step).wait_send()
 
@@ -331,12 +345,13 @@
             return carry
 
         lax.fori_loop(0, slots // PIECES // 4, turn, 0)
-        if piece == PIECES // 2:
+        if piece == PIECES // 4:
             relay(0)
             if chunks > AHEAD:
                 send_own(AHEAD)
 
-    sums[0] = jnp.zeros(sums.shape[1:], jnp.float32)
+    for w in kinds:
+        by_kind[w][2][0] = jnp.zeros((w, TILE), jnp.float32)
 
     for p in range(phases):
         receive(p)
@@ -348,7 +363,6 @@
         if p >= 2:
             settle(p - 2)
         finish(p)
-        acopy(p).start()
         pair_sum(p)
         if p >= 1:
             chip_sum(p - 1)
@@ -361,11 +375,13 @@
 
 
 def filter_bank(coefs, base_ref, first_ref, second_ref, out_ref):
-    base = base_ref[...].astype(jnp.float32)
-    first = first_ref[...].astype(jnp.float32)
-    rest = 2.0 * second_ref[...].astype(jnp.float32) - base
-    for scale, (zero, one, two) in enumerate(coefs):
-        out_ref[scale] = (zero * base + one * first + two * rest).astype(out_ref.dtype)
+    for at in range(0, base_ref.shape[1], TILE):
+        lanes = slice(at, at + TILE)
+        base = base_ref[:, lanes].astype(jnp.float32)
+        first = first_ref[:, lanes].astype(jnp.float32)
+        rest = 2.0 * second_ref[:, lanes].astype(jnp.float32) - base
+        for scale, (zero, one, two) in enumerate(coefs):
+            out_ref[scale, :, lanes] = (zero * base + one * first + two * rest).astype(out_ref.dtype)
 
 
 def shards(features, tile_rows, tile_cols, tile_count, tile_data):
@@ -381,15 +397,15 @@
     widths = [CHUNKS[p % len(CHUNKS)] for p in range(phases)]
     field = jax.ShapeDtypeStruct((channels, nodes), jnp.bfloat16)
     dma = pltpu.SemaphoreType.DMA
-    wide = max(CHUNKS)
     per_block = nodes // TILE
     scratch = [VMEM((row_size * per_block, w, TILE), jnp.bfloat16) for w in widths]
     scratch += [VMEM((chips, per_block, w, TILE), jnp.bfloat16) for w in widths]
     scratch += [VMEM((chips - 1, per_block, w, TILE), jnp.bfloat16) for w in widths]
-    scratch += [VMEM((2, chips, per_block, wide, TILE), jnp.bfloat16)] * 2
+    for w in sorted(set(CHUNKS)):
+        scratch += [VMEM((2, chips, per_block, w, TILE), jnp.bfloat16)] * 2
+        scratch += [VMEM((slots + 1, w, TILE), jnp.float32)]
     scratch += [
         VMEM((slots, TILE, TILE), jnp.bfloat16),
-        VMEM((slots + 1, wide, TILE), jnp.float32),
         VMEM((channels, nodes), jnp.bfloat16),
         VMEM((slots // TILE, TILE), jnp.int32),
         VMEM((slots // TILE, TILE), jnp.float32),
@@ -402,8 +418,8 @@
         dma((PIECES,)),
         dma((phases, 2, 2 * row_size)),
         dma((phases, 2, row_size)),
-        dma((phases,)),
-        dma((phases,)),
+        dma((phases, chips)),
+        dma((phases, chips)),
         dma((phases, chips - 1)),
         dma((phases, chips - 1)),
     ]
@@ -425,7 +441,7 @@
         name="operator_twice",
     )(tile_rows, tile_cols, tile_count, features, slot_data)
 
-    depth = 16
+    depth = 32
     coefs = [tuple(float(c) for c in row) for row in zip(*coefficients())]
     rows = pl.BlockSpec((depth, nodes), lambda i: (i, 0))
     filtered = pl.pallas_call(

time: 99.9 us -> 98.3 us (0.984)
  Pallas kernels: 99.1 us -> 97.4 us
where the time goes in v3:
time: 98.3 us; the launch traced here: 98.1 us
  Pallas kernels  97.4 us (99%)
    pallas_call x1, Pallas kernels, shards(): pl.pallas_call(functools.partial(body, (row_size, col_size, slots, slot_b...  93.1 us
    pallas_call x1, Pallas kernels, shards(): pl.pallas_call(functools.partial(filter_bank, coefs), out_shape=jax.Shape...  4.33 us

profile of v3, /device:TPU:0, one launch (start us, length us, event | category | flops | bytes accessed | tf_op | source)
XLA Modules:
  0.0 98.1 jit_solution(17810469565706604648)
XLA Ops:
  0.7 93.1 %operator_twice.1 = (bf16[64,4096]{1,0:T(8,128)(2,1)}, bf16[64,4096]{1,0:T(8,128)(2,1)}) custom-call(s32[1,1,512]{2,1,0:T(1,128)} %rows_ref.1, s32[1,1,512]{2,1,0:T(1,128)} %cols_ref.1, s32[1,1]{1,0:T(1,128)S(6)} %copy.6.count_ref, bf16[64,4096]{1,0:T(8,128)(2,1)} %base_ref.1, bf16[512,128,128]{2,1,0:T(8,128)(2,1)} %bitcast.2), custom_call_target="tpu_custom_call" | custom-call | tf_op jit(solution)/shard_map/operator_twice/pallas_call | solution.py:426
  93.8 4.3 %filter_bank.1 = bf16[8,64,4096]{2,1,0:T(8,128)(2,1)} custom-call(bf16[64,4096]{1,0:T(8,128)(2,1)} %base_ref.1, bf16[64,4096]{1,0:T(8,128)(2,1)} %get-tuple-element.7.first_ref, bf16[64,4096]{1,0:T(8,128)(2,1)} %get-tuple-element.8.second_ref), custom_call_target="tpu_custom_call" | custom-call | tf_op jit(solution)/shard_map/filter_bank/pallas_call | solution.py:447

commit v4 on v3

--- a/solution.py
+++ b/solution.py
@@ -50,7 +50,7 @@
     arrived_b = [names.pop(0) for _ in range(phases)]
     kinds = sorted(set(CHUNKS))
     by_kind = {w: (names.pop(0), names.pop(0), names.pop(0)) for w in kinds}
-    tiles, field, words, keeps, lasts, meta_ref, keep_ref, last_ref, order_sem, own_sem, tile_sem, zsend, zrecv, asend, arecv, bsend, brecv = names
+    first_held, second_held, out_sem, tiles, field, words, keeps, lasts, meta_ref, keep_ref, last_ref, order_sem, own_sem, tile_sem, zsend, zrecv, asend, arecv, bsend, brecv = names
     width = [CHUNKS[p % chunks] for p in range(phases)]
     start = [sum(CHUNKS[: p % chunks]) for p in range(phases)]
     partials = [by_kind[width[p]][p % 2] for p in range(phases)]
@@ -259,9 +259,15 @@
         if p < chunks:
             panels[p + chunks][pl.ds(me * per_block, per_block)] = result
             send_own(p + chunks)
-        out_ref = first_ref if p < chunks else second_ref
+        out_ref = first_held if p < chunks else second_held
         for block in range(per_block):
             out_ref[start[p] : start[p] + width[p], block * TILE : (block + 1) * TILE] = result[block]
+        out_copy(p).start()
+
+    def out_copy(p):
+        rows = pl.ds(start[p], width[p])
+        held, out = (first_held, first_ref) if p < chunks else (second_held, second_ref)
+        return pltpu.make_async_copy(held.at[rows], out.at[rows], out_sem.at[p])
 
     def settle(p):
         for target in range(chips):
@@ -372,6 +378,7 @@
         settle(p)
     for p in range(phases):
         sent(p)
+        out_copy(p).wait()
 
 
 def filter_bank(coefs, base_ref, first_ref, second_ref, out_ref):
@@ -405,6 +412,9 @@
         scratch += [VMEM((2, chips, per_block, w, TILE), jnp.bfloat16)] * 2
         scratch += [VMEM((slots + 1, w, TILE), jnp.float32)]
     scratch += [
+        VMEM((channels, nodes), jnp.bfloat16),
+        VMEM((channels, nodes), jnp.bfloat16),
+        dma((phases,)),
         VMEM((slots, TILE, TILE), jnp.bfloat16),
         VMEM((channels, nodes), jnp.bfloat16),
         VMEM((slots // TILE, TILE), jnp.int32),
@@ -433,7 +443,7 @@
             pl.BlockSpec(memory_space=pl.ANY),
             pl.BlockSpec(memory_space=pl.ANY),
         ],
-        out_specs=(pl.BlockSpec(memory_space=VMEM), pl.BlockSpec(memory_space=VMEM)),
+        out_specs=(pl.BlockSpec(memory_space=pl.ANY), pl.BlockSpec(memory_space=pl.ANY)),
         scratch_shapes=scratch,
         compiler_params=pltpu.CompilerParams(
             collective_id=0, has_side_effects=True, vmem_limit_bytes=60 * 2**20

time: 98.3 us -> 97.9 us (level)
  no operation moved by 1% of the time
where the time goes in v4:
time: 97.9 us; the launch traced here: 97.7 us
  Pallas kernels  97.1 us (99%)
    pallas_call x1, Pallas kernels, shards(): pl.pallas_call(functools.partial(body, (row_size, col_size, slots, slot_b...  92.7 us
    pallas_call x1, Pallas kernels, shards(): pl.pallas_call(functools.partial(filter_bank, coefs), out_shape=jax.Shape...  4.33 us

profile of v4, /device:TPU:0, one launch (start us, length us, event | category | flops | bytes accessed | tf_op | source)
XLA Modules:
  0.0 97.7 jit_solution(12465752326059429581)
XLA Ops:
  0.7 92.7 %operator_twice.1 = (bf16[64,4096]{1,0:T(8,128)(2,1)}, bf16[64,4096]{1,0:T(8,128)(2,1)}) custom-call(s32[1,1,512]{2,1,0:T(1,128)} %rows_ref.1, s32[1,1,512]{2,1,0:T(1,128)} %cols_ref.1, s32[1,1]{1,0:T(1,128)S(6)} %copy.6.count_ref, bf16[64,4096]{1,0:T(8,128)(2,1)} %base_ref.1, bf16[512,128,128]{2,1,0:T(8,128)(2,1)} %bitcast.2), custom_call_target="tpu_custom_call" | custom-call | tf_op jit(solution)/shard_map/operator_twice/pallas_call | solution.py:436
  93.4 4.3 %filter_bank.1 = bf16[8,64,4096]{2,1,0:T(8,128)(2,1)} custom-call(bf16[64,4096]{1,0:T(8,128)(2,1)} %base_ref.1, bf16[64,4096]{1,0:T(8,128)(2,1)} %get-tuple-element.7.first_ref, bf16[64,4096]{1,0:T(8,128)(2,1)} %get-tuple-element.8.second_ref), custom_call_target="tpu_custom_call" | custom-call | tf_op jit(solution)/shard_map/filter_bank/pallas_call | solution.py:457
